TPU v7x, 256 devices: a whole 4x4x8 slice. The times are simulated.
256 devices in a mesh: wave: 16 (over z, y_hi), lat: 16 (over x, y_lo, core).
Axes of the slice: x: 4, y: 4 (y_hi: 2, y_lo: 2; y = y_hi * 2 + y_lo), z: 8, core: 2. Of those that a mesh axis runs over, the one named last changes fastest.
Arguments:
- control: bfloat16 [640, 640, 256], P('wave', 'lat'), may hold values from -6 to 6
- vert_root: bfloat16 [640, 128, 128], P('wave'), may hold values from -0.5 to 0.5
- legendre: bfloat16 [640, 640, 256], P('lat', 'wave'), may hold values from -0.3125 to 0.3125
- row_wavenumber: int32 [640], P('wave'), may hold values from 0 to 639, each once
- courant_east: float32 [256, 1280, 128], P('wave', 'lat'), may hold values from 0.05 to 0.45
- courant_north: float32 [256, 1280, 128], P('wave', 'lat'), may hold values from 0.05 to 0.45
- east_flags: int32 [256, 1280, 128], P('wave', 'lat'), may hold values 0 or 1
- north_flags: int32 [256, 1280, 128], P('wave', 'lat'), may hold values 0 or 1
Outputs:
- tracer: float32 [256, 1280, 128], P('wave', 'lat')
Inputs may be any that keep to these rules, and one draw needn't show every extreme that they name: `row_wavenumber`: A permutation of 0 to 639.
All inputs are finite; a program needn't handle non-finite values. No bound on the sum of `east_flags` or of `north_flags` on one device may be relied on, other than what follows from the above.
Results may differ from a plain program's by a relative error of at most 0.0069.
Values may be sent and summed in bfloat16 or wider, within the bound.
No kernel may reach another device: no remote copies, remote signals or barrier semaphores. Data moves between devices by JAX's collectives and lax.ppermute only.
A program may use at most 64 MiB of HBM per device.

v0:
```python
import math
import jax
import jax.numpy as jnp
from jax import lax
from jax.sharding import PartitionSpec as P

LEV = 128
STEPS = 4


def cut_along(array, dim, length):
    shape = array.shape
    blocks = array.reshape(*shape[:dim], length, shape[dim] // length, *shape[dim + 1 :])
    return jnp.moveaxis(blocks, dim, 0)


def sum_at_owner(array, axis, dim):
    length = lax.axis_size(axis)
    blocks = lax.all_to_all(cut_along(array, dim, length), axis, 0, 0, tiled=True)
    return jnp.sum(blocks.astype(jnp.float32), axis=0)


def passed_along(value, axis, steps):
    count = lax.axis_size(axis)
    pairs = [(source, (source + steps) % count) for source in range(count)]
    return lax.ppermute(value, axis, pairs)


def passed_along_2(block, axis, distance):
    devices = range(lax.axis_size(axis))
    route = [(i - distance, i) for i in devices if i - distance in devices]
    return lax.ppermute(block, axis, route)


def with_halo(array, sides, width, wrap):
    for axis, dim in sides:
        size, length = (lax.axis_size(axis), array.shape[dim])
        up = [(i, (i + 1) % size) for i in range(size if wrap else size - 1)]
        down = [(j, i) for i, j in up]
        last = lax.slice_in_dim(array, length - width, length, axis=dim)
        leading = lax.slice_in_dim(array, 0, width, axis=dim)
        before = lax.ppermute(last, axis, up)
        after = lax.ppermute(leading, axis, down)
        array = jnp.concatenate([before, array, after], axis=dim)
    return array


def minmod(first_jump, second_jump):
    return jnp.maximum(0.0, jnp.minimum(first_jump, second_jump)) + jnp.minimum(
        0.0, jnp.maximum(first_jump, second_jump)
    )


def window(values, begin_at, end_at, axis_dim):
    return lax.slice_in_dim(values, begin_at, end_at, axis=axis_dim)


def transport(padded, winds, axis_dim, cell_count):
    jumps = window(padded, 1, cell_count + 4, axis_dim) - window(
        padded, 0, cell_count + 3, axis_dim
    )
    limited = minmod(
        window(jumps, 1, cell_count + 3, axis_dim), window(jumps, 0, cell_count + 2, axis_dim)
    )
    below_cells = window(padded, 1, cell_count + 2, axis_dim)
    above_cells = window(padded, 2, cell_count + 3, axis_dim)
    lower_slope = window(limited, 0, cell_count + 1, axis_dim)
    upper_slope = window(limited, 1, cell_count + 2, axis_dim)
    courant = jnp.abs(winds)
    fluxes = jnp.maximum(winds, 0.0) * (
        below_cells + 0.5 * (1.0 - courant) * lower_slope
    ) + jnp.minimum(winds, 0.0) * (above_cells - 0.5 * (1.0 - courant) * upper_slope)
    return window(fluxes, 1, cell_count + 1, axis_dim) - window(fluxes, 0, cell_count, axis_dim)


def dft_basis(order_ids, lon_ids, total_lon, total_orders):
    product = order_ids[:, None] * lon_ids[None, :] % total_lon
    phases = product.astype(jnp.float32) * (2.0 * math.pi / total_lon)
    weight = jnp.where(order_ids == 0, 1.0, 2.0).astype(jnp.float32) * (
        1.0 / math.sqrt(2.0 * total_orders)
    )
    return jnp.stack(
        [weight[:, None] * jnp.cos(phases), -weight[:, None] * jnp.sin(phases)]
    ).astype(jnp.bfloat16)


def per_device(
    control,
    vert_root,
    legendre,
    row_wavenumber,
    courant_east,
    courant_north,
    east_flags,
    north_flags,
):
    row_count, order_count, double_levels = control.shape
    wave_count = lax.axis_size("wave")
    lat_count = lax.axis_size("lat")
    total_orders = order_count * lat_count
    total_lon = 2 * total_orders
    level_local = LEV // wave_count
    latitudes = legendre.shape[2]
    orders = lax.axis_index("lat") * order_count + jnp.arange(order_count, dtype=jnp.int32)
    exists = row_wavenumber[:, None] >= orders[None, :]
    spectra = jnp.where(exists[:, :, None], control, jnp.zeros((), control.dtype))
    complex_parts = spectra.reshape(row_count, order_count, LEV, 2)
    vertical = jnp.einsum(
        "rmlp,rkl->kpmr", complex_parts, vert_root, preferred_element_type=jnp.float32
    ).astype(jnp.bfloat16)
    stacked = vertical.reshape(2 * LEV, order_count, row_count)
    segment = stacked
    modes_sum = sum_at_owner(
        jnp.einsum("cmr,mrj->cmj", segment, legendre, preferred_element_type=jnp.float32).astype(
            jnp.bfloat16
        ),
        "wave",
        0,
    )
    latitude_modes = modes_sum.astype(jnp.bfloat16)
    lon_local = total_lon // lat_count
    lon_ids = lax.axis_index("lat") * lon_local + jnp.arange(lon_local, dtype=jnp.int32)
    segment = lax.all_gather(latitude_modes, "lat", axis=1, tiled=True)
    order_ids = jnp.arange(segment.shape[1], dtype=jnp.int32)
    basis = dft_basis(order_ids, lon_ids, total_lon, total_orders)
    shaped = segment.reshape(level_local, 2, segment.shape[1], latitudes)
    gridded = jnp.einsum("kpmj,pml->jlk", shaped, basis, preferred_element_type=jnp.float32)
    column_tile = lax.all_to_all(gridded, "wave", split_axis=0, concat_axis=2, tiled=True)
    wind_east = courant_east * (2 * east_flags - 1).astype(jnp.float32)
    wind_north = courant_north * (2 * north_flags - 1).astype(jnp.float32)
    west_edge = passed_along(wind_east[:, -1:], "lat", 1)
    winds_x = jnp.concatenate([west_edge, wind_east], axis=1)
    south_edge = passed_along_2(wind_north[-1:], "wave", 1)
    winds_y = jnp.concatenate([south_edge, wind_north], axis=0)
    tracer = column_tile
    tile_rows = tracer.shape[0]
    tile_lon = tracer.shape[1]
    for repeat in range(STEPS):
        lon_padded = with_halo(tracer.astype(jnp.bfloat16), (("lat", 1),), 2, True).astype(
            tracer.dtype
        )
        row_padded = with_halo(tracer.astype(jnp.bfloat16), (("wave", 0),), 2, False).astype(
            tracer.dtype
        )
        tracer = (
            tracer
            - transport(lon_padded, winds_x, 1, tile_lon)
            - transport(row_padded, winds_y, 0, tile_rows)
        )
    return tracer


def solution(mesh):
    return jax.shard_map(
        per_device,
        mesh=mesh,
        in_specs=(
            P("wave", "lat", None),
            P("wave", None, None),
            P("lat", "wave", None),
            P("wave"),
            P("wave", "lat", None),
            P("wave", "lat", None),
            P("wave", "lat", None),
            P("wave", "lat", None),
        ),
        out_specs=P("wave", "lat", None),
        check_vma=False,
    )
```

profile of v0, /device:TPU:64, one launch (start us, length us, event | category | flops | bytes accessed | tf_op | source)
XLA Modules:
  0.0 311.1 jit_solution(2980356625274923959)
XLA Ops:
  7.4 1.4 broadcast_select_fusion
  8.8 4.0 %copy.54 = bf16[40,40,256]{1,0,2:T(8,128)(2,1)} copy(bf16[40,40,256]{2,1,0:T(8,128)(2,1)S(1)} %broadcast_select_fusion) | data formatting | bytes 1638400 | tf_op jit(solution)/shard_map/jit(_where)/select_n | solution.py:106
  12.8 2.7 fusion.7
  15.5 5.8 %copy.56 = bf16[128,2,40,40]{3,2,1,0:T(8,128)(2,1)} copy(bf16[128,2,40,40]{0,2,1,3:T(8,128)(2,1)S(1)} %fusion.7) | data formatting | bytes 1638400 | tf_op jit(solution)/shard_map/convert_element_type | solution.py:110
  21.3 3.3 %convolution_convert_fusion = bf16[40,256,256]{2,1,0:T(8,128)(2,1)S(1)} fusion(bf16[40,40,256]{2,1,0:T(8,128)(2,1)S(1)} %copy-done.2, bf16[256,40,40]{2,1,0:T(8,128)(2,1)} %bitcast.36), kind=kOutput, calls=%fused_computation | convolution fusion | flops 212336640 | bytes 6881280 | tf_op jit(solution)/shard_map/cmr,mrj->cmj/dot_general | solution.py:114
  25.1 128.6 %all_to_all.23 = bf16[16,16,40,256]{3,1,2,0:T(8,128)(2,1)} all-to-all(bf16[16,16,40,256]{3,1,2,0:T(8,128)(2,1)S(1)} %copy.58), channel_id=1, replica_groups=mesh['wave'=16,'lat'=16] {'wave'}, dimensions={0} | all-to-all | bytes 10485760 | tf_op jit(solution)/shard_map/all_to_all | solution.py:19
  153.7 4.0 %reduce_sum.12 = bf16[16,40,256]{2,0,1:T(8,128)(2,1)} reduce(bf16[16,16,40,256]{3,1,2,0:T(8,128)(2,1)} %all_to_all.23, bf16[]{:T(256)} %constant.23.clone.1), dimensions={0}, to_apply=%region_0.1 | reduce | flops 2457600 | bytes 5570562 | tf_op jit(solution)/shard_map/reduce_sum | solution.py:20
  158.7 37.5 %all-gather.2.cloned.1.call-done = bf16[16,640,256]{2,0,1:T(8,128)(2,1)} async-done(((bf16[16,40,256]{2,0,1:T(8,128)(2,1)}), bf16[16,640,256]{2,0,1:T(8,128)(2,1)}) %all-gather.2.cloned.1.call-update) | async-done | bytes 5242896 | tf_op jit(solution)/shard_map/all_gather | solution.py:123
  196.2 4.3 %copy.60 = bf16[16,640,256]{2,1,0:T(8,128)(2,1)S(1)} copy(bf16[16,640,256]{2,0,1:T(8,128)(2,1)} %all-gather.2.cloned.1.call-done) | data formatting | bytes 10485760 | tf_op jit(solution)/shard_map/all_gather | solution.py:123
  201.6 1.3 copy.61
  202.9 9.8 %all-to-all-start.1 = ((f32[256,80,8]{1,2,0:T(8,128)}), f32[256,80,8]{1,2,0:T(8,128)S(1)}, u32[]{:S(2)}, u32[]{:S(2)}) async-start(f32[256,80,8]{1,2,0:T(8,128)} %copy.61), calls=%async_computation.1 | async-start | bytes 2097152 | tf_op jit(solution)/shard_map/all_to_all | solution.py:128
  212.7 1.2 convert_multiply_fusion
  213.9 4.9 %collective-permute-start.3 = (f32[1,80,128]{2,1,0:T(8,128)S(1)}, f32[1,80,128]{2,1,0:T(8,128)S(1)}, u32[]{:S(2)}, u32[]{:S(2)}) collective-permute-start(f32[1,80,128]{2,1,0:T(8,128)S(1)} %slice.405), channel_id=1, source_target_pairs={{0,16},{16,32},{32,48},{48,64},{64,80},{80,96},{96,112},{112,128},... | collective-permute-start | bytes 122888 | tf_op jit(solution)/shard_map/ppermute | solution.py:32
  218.8 1.4 convert_multiply_fusion.1
  220.3 21.5 %all-to-all-done.1 = f32[256,80,8]{1,2,0:T(8,128)S(1)} async-done(((f32[256,80,8]{1,2,0:T(8,128)}), f32[256,80,8]{1,2,0:T(8,128)S(1)}, u32[]{:S(2)}, u32[]{:S(2)}) %all-to-all-start.1) | async-done | bytes 655392 | tf_op jit(solution)/shard_map/all_to_all | solution.py:128
  241.7 1.1 copy.79
  242.8 1.5 copy.66
  245.2 1.9 collective-permute-start.5
  247.2 5.4 %collective-permute-start.4 = (bf16[2,80,128]{2,1,0:T(8,128)(2,1)S(1)}, bf16[2,80,128]{2,1,0:T(8,128)(2,1)S(1)}, u32[]{:S(2)}, u32[]{:S(2)}) collective-permute-start(bf16[2,80,128]{2,1,0:T(8,128)(2,1)S(1)} %get-tuple-element.25), channel_id=1, source_target_pairs={{0,16},{16,32},{32,48},{48,64},{64,80},{80,96},{96,112},{112,128},... | collective-permute-start | bytes 122888 | tf_op jit(solution)/shard_map/ppermute | solution.py:42
  253.5 2.1 collective-permute-done.4
  256.4 2.5 collective-permute-start.7
  258.9 3.3 %collective-permute-start.9 = (bf16[2,80,128]{2,1,0:T(8,128)(2,1)S(1)}, bf16[2,80,128]{2,1,0:T(8,128)(2,1)S(1)}, u32[]{:S(2)}, u32[]{:S(2)}) collective-permute-start(bf16[2,80,128]{2,1,0:T(8,128)(2,1)S(1)} %get-tuple-element.22), channel_id=1, source_target_pairs={{16,0},{32,16},{48,32},{64,48},{80,64},{96,80},{112,96},{128,112},... | collective-permute-start | bytes 122888 | tf_op jit(solution)/shard_map/ppermute | solution.py:43
  262.2 4.1 %collective-permute-start.8 = (bf16[2,80,128]{2,1,0:T(8,128)(2,1)S(1)}, bf16[2,80,128]{2,1,0:T(8,128)(2,1)S(1)}, u32[]{:S(2)}, u32[]{:S(2)}) collective-permute-start(bf16[2,80,128]{2,1,0:T(8,128)(2,1)S(1)} %get-tuple-element.21), channel_id=1, source_target_pairs={{0,16},{16,32},{32,48},{48,64},{64,80},{80,96},{96,112},{112,128},... | collective-permute-start | bytes 122888 | tf_op jit(solution)/shard_map/ppermute | solution.py:42
  267.2 3.3 %collective-permute-done.8 = bf16[2,80,128]{2,1,0:T(8,128)(2,1)S(1)} collective-permute-done((bf16[2,80,128]{2,1,0:T(8,128)(2,1)S(1)}, bf16[2,80,128]{2,1,0:T(8,128)(2,1)S(1)}, u32[]{:S(2)}, u32[]{:S(2)}) %collective-permute-start.8) | collective-permute-done | bytes 40992 | tf_op jit(solution)/shard_map/ppermute | solution.py:42
  271.3 1.9 collective-permute-start.11
  273.2 4.9 %collective-permute-start.13 = (bf16[2,80,128]{2,1,0:T(8,128)(2,1)S(1)}, bf16[2,80,128]{2,1,0:T(8,128)(2,1)S(1)}, u32[]{:S(2)}, u32[]{:S(2)}) collective-permute-start(bf16[2,80,128]{2,1,0:T(8,128)(2,1)S(1)} %get-tuple-element.18), channel_id=1, source_target_pairs={{16,0},{32,16},{48,32},{64,48},{80,64},{96,80},{112,96},{128,112},... | collective-permute-start | bytes 122888 | tf_op jit(solution)/shard_map/ppermute | solution.py:43
  278.1 2.4 collective-permute-start.12
  281.4 5.0 %collective-permute-done.12 = bf16[2,80,128]{2,1,0:T(8,128)(2,1)S(1)} collective-permute-done((bf16[2,80,128]{2,1,0:T(8,128)(2,1)S(1)}, bf16[2,80,128]{2,1,0:T(8,128)(2,1)S(1)}, u32[]{:S(2)}, u32[]{:S(2)}) %collective-permute-start.12) | collective-permute-done | bytes 40992 | tf_op jit(solution)/shard_map/ppermute | solution.py:42
  287.2 1.9 collective-permute-start.15
  289.1 5.3 %collective-permute-start.17 = (bf16[2,80,128]{2,1,0:T(8,128)(2,1)S(1)}, bf16[2,80,128]{2,1,0:T(8,128)(2,1)S(1)}, u32[]{:S(2)}, u32[]{:S(2)}) collective-permute-start(bf16[2,80,128]{2,1,0:T(8,128)(2,1)S(1)} %get-tuple-element.14), channel_id=1, source_target_pairs={{16,0},{32,16},{48,32},{64,48},{80,64},{96,80},{112,96},{128,112},... | collective-permute-start | bytes 122888 | tf_op jit(solution)/shard_map/ppermute | solution.py:43
  294.4 2.0 collective-permute-start.16
  297.3 5.4 %collective-permute-done.16 = bf16[2,80,128]{2,1,0:T(8,128)(2,1)S(1)} collective-permute-done((bf16[2,80,128]{2,1,0:T(8,128)(2,1)S(1)}, bf16[2,80,128]{2,1,0:T(8,128)(2,1)S(1)}, u32[]{:S(2)}, u32[]{:S(2)}) %collective-permute-start.16) | collective-permute-done | bytes 40992 | tf_op jit(solution)/shard_map/ppermute | solution.py:42
  (84 shorter events, 11.5 us)
Async XLA Ops:
  6.5 6.3 %copy-start = (bf16[40,128,128]{2,1,0:T(8,128)(2,1)S(1)}, bf16[40,128,128]{2,1,0:T(8,128)(2,1)}, u32[]{:S(2)}) copy-start(bf16[40,128,128]{2,1,0:T(8,128)(2,1)} %param.9) | copy-start | bytes 3932164
  6.5 189.7 %all-gather.2.cloned.1.call-start = ((), (), s32[]{:S(2)}) async-start(), calls=%async_computation.2 | async-start | bytes 5570560 | tf_op jit(solution)/shard_map/all_gather | solution.py:123
  15.5 5.8 %copy-start.2 = (bf16[40,40,256]{2,1,0:T(8,128)(2,1)S(1)}, bf16[40,40,256]{2,1,0:T(8,128)(2,1)}, u32[]{:S(2)}) copy-start(bf16[40,40,256]{2,1,0:T(8,128)(2,1)} %param.10) | copy-start | bytes 2457604
  201.6 11.1 %copy-start.3 = (f32[16,80,128]{2,1,0:T(8,128)S(1)}, f32[16,80,128]{2,1,0:T(8,128)}, u32[]{:S(2)}) copy-start(f32[16,80,128]{2,1,0:T(8,128)} %param.13) | copy-start | bytes 1966084
  202.9 38.8 %all-to-all-start.1 = ((f32[256,80,8]{1,2,0:T(8,128)}), f32[256,80,8]{1,2,0:T(8,128)S(1)}, u32[]{:S(2)}, u32[]{:S(2)}) async-start(f32[256,80,8]{1,2,0:T(8,128)} %copy.61), calls=%async_computation.1 | async-start | bytes 2097152 | tf_op jit(solution)/shard_map/all_to_all | solution.py:128
  213.9 41.9 %collective-permute-start.3 = (f32[1,80,128]{2,1,0:T(8,128)S(1)}, f32[1,80,128]{2,1,0:T(8,128)S(1)}, u32[]{:S(2)}, u32[]{:S(2)}) collective-permute-start(f32[1,80,128]{2,1,0:T(8,128)S(1)} %slice.405), channel_id=1, source_target_pairs={{0,16},{16,32},{32,48},{48,64},{64,80},{80,96},{96,112},{112,128},... | collective-permute-start | bytes 122888 | tf_op jit(solution)/shard_map/ppermute | solution.py:32
  220.2 32.8 %collective-permute-start = (f32[16,1,128]{2,0,1:T(8,128)S(1)}, f32[16,1,128]{2,0,1:T(8,128)S(1)}, u32[]{:S(2)}, u32[]{:S(2)}) collective-permute-start(f32[16,1,128]{2,0,1:T(8,128)S(1)} %bitcast.43), channel_id=1, source_target_pairs={{0,1},{1,2},{2,3},{3,4},{4,5},{5,6},{6,7},{7,8},{8,9},{9,10},{10,1... | collective-permute-start | bytes 24584 | tf_op jit(solution)/shard_map/ppermute | solution.py:26
  244.5 2.7 collective-permute-start.2
  245.1 7.5 %collective-permute-start.1 = (bf16[16,2,128]{2,1,0:T(2,128)(2,1)S(1)}, bf16[16,2,128]{2,1,0:T(2,128)(2,1)S(1)}, u32[]{:S(2)}, u32[]{:S(2)}) collective-permute-start(bf16[16,2,128]{2,1,0:T(2,128)(2,1)S(1)} %get-tuple-element.23), channel_id=1, source_target_pairs={{0,1},{1,2},{2,3},{3,4},{4,5},{5,6},{6,7},{7,8},{8,9},{9,10},{10,1... | collective-permute-start | bytes 24584 | tf_op jit(solution)/shard_map/ppermute | solution.py:42
  245.2 8.2 %collective-permute-start.5 = (bf16[2,80,128]{2,1,0:T(8,128)(2,1)S(1)}, bf16[2,80,128]{2,1,0:T(8,128)(2,1)S(1)}, u32[]{:S(2)}, u32[]{:S(2)}) collective-permute-start(bf16[2,80,128]{2,1,0:T(8,128)(2,1)S(1)} %get-tuple-element.26), channel_id=1, source_target_pairs={{16,0},{32,16},{48,32},{64,48},{80,64},{96,80},{112,96},{128,112},... | collective-permute-start | bytes 122888 | tf_op jit(solution)/shard_map/ppermute | solution.py:43
  247.2 8.4 %collective-permute-start.4 = (bf16[2,80,128]{2,1,0:T(8,128)(2,1)S(1)}, bf16[2,80,128]{2,1,0:T(8,128)(2,1)S(1)}, u32[]{:S(2)}, u32[]{:S(2)}) collective-permute-start(bf16[2,80,128]{2,1,0:T(8,128)(2,1)S(1)} %get-tuple-element.25), channel_id=1, source_target_pairs={{0,16},{16,32},{32,48},{48,64},{64,80},{80,96},{96,112},{112,128},... | collective-permute-start | bytes 122888 | tf_op jit(solution)/shard_map/ppermute | solution.py:42
  256.4 9.9 %collective-permute-start.7 = (bf16[16,2,128]{2,1,0:T(2,128)(2,1)S(1)}, bf16[16,2,128]{2,1,0:T(2,128)(2,1)S(1)}, u32[]{:S(2)}, u32[]{:S(2)}) collective-permute-start(bf16[16,2,128]{2,1,0:T(2,128)(2,1)S(1)} %get-tuple-element.20), channel_id=1, source_target_pairs={{1,0},{2,1},{3,2},{4,3},{5,4},{6,5},{7,6},{8,7},{9,8},{10,9},{11,1... | collective-permute-start | bytes 24584 | tf_op jit(solution)/shard_map/ppermute | solution.py:43
  258.9 7.4 %collective-permute-start.6 = (bf16[16,2,128]{2,1,0:T(2,128)(2,1)S(1)}, bf16[16,2,128]{2,1,0:T(2,128)(2,1)S(1)}, u32[]{:S(2)}, u32[]{:S(2)}) collective-permute-start(bf16[16,2,128]{2,1,0:T(2,128)(2,1)S(1)} %get-tuple-element.19), channel_id=1, source_target_pairs={{0,1},{1,2},{2,3},{3,4},{4,5},{5,6},{6,7},{7,8},{8,9},{9,10},{10,1... | collective-permute-start | bytes 24584 | tf_op jit(solution)/shard_map/ppermute | solution.py:42
  258.9 8.2 %collective-permute-start.9 = (bf16[2,80,128]{2,1,0:T(8,128)(2,1)S(1)}, bf16[2,80,128]{2,1,0:T(8,128)(2,1)S(1)}, u32[]{:S(2)}, u32[]{:S(2)}) collective-permute-start(bf16[2,80,128]{2,1,0:T(8,128)(2,1)S(1)} %get-tuple-element.22), channel_id=1, source_target_pairs={{16,0},{32,16},{48,32},{64,48},{80,64},{96,80},{112,96},{128,112},... | collective-permute-start | bytes 122888 | tf_op jit(solution)/shard_map/ppermute | solution.py:43
  262.2 8.3 %collective-permute-start.8 = (bf16[2,80,128]{2,1,0:T(8,128)(2,1)S(1)}, bf16[2,80,128]{2,1,0:T(8,128)(2,1)S(1)}, u32[]{:S(2)}, u32[]{:S(2)}) collective-permute-start(bf16[2,80,128]{2,1,0:T(8,128)(2,1)S(1)} %get-tuple-element.21), channel_id=1, source_target_pairs={{0,16},{16,32},{32,48},{48,64},{64,80},{80,96},{96,112},{112,128},... | collective-permute-start | bytes 122888 | tf_op jit(solution)/shard_map/ppermute | solution.py:42
  271.3 9.3 %collective-permute-start.11 = (bf16[16,2,128]{2,1,0:T(2,128)(2,1)S(1)}, bf16[16,2,128]{2,1,0:T(2,128)(2,1)S(1)}, u32[]{:S(2)}, u32[]{:S(2)}) collective-permute-start(bf16[16,2,128]{2,1,0:T(2,128)(2,1)S(1)} %get-tuple-element.16), channel_id=1, source_target_pairs={{1,0},{2,1},{3,2},{4,3},{5,4},{6,5},{7,6},{8,7},{9,8},{10,9},{11,1... | collective-permute-start | bytes 24584 | tf_op jit(solution)/shard_map/ppermute | solution.py:43
  273.2 7.4 %collective-permute-start.10 = (bf16[16,2,128]{2,1,0:T(2,128)(2,1)S(1)}, bf16[16,2,128]{2,1,0:T(2,128)(2,1)S(1)}, u32[]{:S(2)}, u32[]{:S(2)}) collective-permute-start(bf16[16,2,128]{2,1,0:T(2,128)(2,1)S(1)} %get-tuple-element.15), channel_id=1, source_target_pairs={{0,1},{1,2},{2,3},{3,4},{4,5},{5,6},{6,7},{7,8},{8,9},{9,10},{10,1... | collective-permute-start | bytes 24584 | tf_op jit(solution)/shard_map/ppermute | solution.py:42
  273.2 8.2 %collective-permute-start.13 = (bf16[2,80,128]{2,1,0:T(8,128)(2,1)S(1)}, bf16[2,80,128]{2,1,0:T(8,128)(2,1)S(1)}, u32[]{:S(2)}, u32[]{:S(2)}) collective-permute-start(bf16[2,80,128]{2,1,0:T(8,128)(2,1)S(1)} %get-tuple-element.18), channel_id=1, source_target_pairs={{16,0},{32,16},{48,32},{64,48},{80,64},{96,80},{112,96},{128,112},... | collective-permute-start | bytes 122888 | tf_op jit(solution)/shard_map/ppermute | solution.py:43
  278.1 8.3 %collective-permute-start.12 = (bf16[2,80,128]{2,1,0:T(8,128)(2,1)S(1)}, bf16[2,80,128]{2,1,0:T(8,128)(2,1)S(1)}, u32[]{:S(2)}, u32[]{:S(2)}) collective-permute-start(bf16[2,80,128]{2,1,0:T(8,128)(2,1)S(1)} %get-tuple-element.17), channel_id=1, source_target_pairs={{0,16},{16,32},{32,48},{48,64},{64,80},{80,96},{96,112},{112,128},... | collective-permute-start | bytes 122888 | tf_op jit(solution)/shard_map/ppermute | solution.py:42
  287.2 9.3 %collective-permute-start.15 = (bf16[16,2,128]{2,1,0:T(2,128)(2,1)S(1)}, bf16[16,2,128]{2,1,0:T(2,128)(2,1)S(1)}, u32[]{:S(2)}, u32[]{:S(2)}) collective-permute-start(bf16[16,2,128]{2,1,0:T(2,128)(2,1)S(1)} %get-tuple-element.12), channel_id=1, source_target_pairs={{1,0},{2,1},{3,2},{4,3},{5,4},{6,5},{7,6},{8,7},{9,8},{10,9},{11,1... | collective-permute-start | bytes 24584 | tf_op jit(solution)/shard_map/ppermute | solution.py:43
  289.1 7.4 %collective-permute-start.14 = (bf16[16,2,128]{2,1,0:T(2,128)(2,1)S(1)}, bf16[16,2,128]{2,1,0:T(2,128)(2,1)S(1)}, u32[]{:S(2)}, u32[]{:S(2)}) collective-permute-start(bf16[16,2,128]{2,1,0:T(2,128)(2,1)S(1)} %get-tuple-element.11), channel_id=1, source_target_pairs={{0,1},{1,2},{2,3},{3,4},{4,5},{5,6},{6,7},{7,8},{8,9},{9,10},{10,1... | collective-permute-start | bytes 24584 | tf_op jit(solution)/shard_map/ppermute | solution.py:42
  289.1 8.2 %collective-permute-start.17 = (bf16[2,80,128]{2,1,0:T(8,128)(2,1)S(1)}, bf16[2,80,128]{2,1,0:T(8,128)(2,1)S(1)}, u32[]{:S(2)}, u32[]{:S(2)}) collective-permute-start(bf16[2,80,128]{2,1,0:T(8,128)(2,1)S(1)} %get-tuple-element.14), channel_id=1, source_target_pairs={{16,0},{32,16},{48,32},{64,48},{80,64},{96,80},{112,96},{128,112},... | collective-permute-start | bytes 122888 | tf_op jit(solution)/shard_map/ppermute | solution.py:43
  294.4 8.3 %collective-permute-start.16 = (bf16[2,80,128]{2,1,0:T(8,128)(2,1)S(1)}, bf16[2,80,128]{2,1,0:T(8,128)(2,1)S(1)}, u32[]{:S(2)}, u32[]{:S(2)}) collective-permute-start(bf16[2,80,128]{2,1,0:T(8,128)(2,1)S(1)} %get-tuple-element.13), channel_id=1, source_target_pairs={{0,16},{16,32},{32,48},{48,64},{64,80},{80,96},{96,112},{112,128},... | collective-permute-start | bytes 122888 | tf_op jit(solution)/shard_map/ppermute | solution.py:42
  303.0 1.3 copy-start.1
Sparse Core Ops, SparseCore 0:
  157.9 38.2 all-gather.1
where the time goes:
time: 312 us; the launch traced here: 311 us
  blocking collectives  129 us (41%)
  waiting for transfers between devices  74.9 us (24%)
  starting transfers between devices  51.2 us (16%)
  local copies, waits for them, and re-layouts  18.7 us (6%)
  other arithmetic  16.8 us (5%)
  between operations  14 us (4%)
  matrix products  6.99 us (2%)
    all_to_all x1, blocking collectives, sum_at_owner(): lax.all_to_all(cut_along(array, dim, length), axis, 0, 0, tiled=True)  129 us
    all_gather x1, waiting for transfers between devices, per_device(): segment = lax.all_gather(latitude_modes, 'lat', axis=1, tiled=True)  37.5 us
    ppermute x8, starting transfers between devices, with_halo(): after = lax.ppermute(leading, axis, down)  22.4 us
    all_to_all x1, waiting for transfers between devices, per_device(): lax.all_to_all(gridded, 'wave', split_axis=0, concat_axis=2, tiled=True)  21.5 us
    ppermute x8, waiting for transfers between devices, with_halo(): before = lax.ppermute(last, axis, up)  15.9 us
    ppermute x8, starting transfers between devices, with_halo(): before = lax.ppermute(last, axis, up)  14.1 us
    all_to_all x1, starting transfers between devices, per_device(): lax.all_to_all(gridded, 'wave', split_axis=0, concat_axis=2, tiled=True)  9.8 us
  transfers between devices with their start and end apart: 20, of which 6 were waited for; matrix products, arithmetic and copies ran while one was open for 3% of the time, Pallas kernels for 0%

commit v1 on v0

--- a/solution.py
+++ b/solution.py
@@ -120,7 +120,9 @@
     latitude_modes = modes_sum.astype(jnp.bfloat16)
     lon_local = total_lon // lat_count
     lon_ids = lax.axis_index("lat") * lon_local + jnp.arange(lon_local, dtype=jnp.int32)
-    segment = lax.all_gather(latitude_modes, "lat", axis=1, tiled=True)
+    segment = jnp.concatenate(
+        lax.all_to_all(jnp.stack([latitude_modes] * lax.axis_size("lat")), "lat", 0, 0), axis=1
+    )
     order_ids = jnp.arange(segment.shape[1], dtype=jnp.int32)
     basis = dft_basis(order_ids, lon_ids, total_lon, total_orders)
     shaped = segment.reshape(level_local, 2, segment.shape[1], latitudes)

time: 312 us -> 339 us (1.087)
  waiting for transfers between devices: 74.9 us -> 113 us
  between operations: 14 us -> 0.6 us
    all_to_all x0 -> x1, waiting for transfers between devices: none -> 75.2 us  [per_device(): lax.all_to_all(jnp.stack([latitude_modes] * lax.axis_size('lat')), 'lat',...]
    all_gather x1 -> x0, waiting for transfers between devices: 37.5 us -> none  [per_device(): segment = lax.all_gather(latitude_modes, 'lat', axis=1, tiled=True)]
    all_to_all x0 -> x1, starting transfers between devices: none -> 4.59 us  [per_device(): lax.all_to_all(jnp.stack([latitude_modes] * lax.axis_size('lat')), 'lat',...]
    all_gather x1 -> x0, local copies, waits for them, and re-layouts: 4.34 us -> none  [per_device(): segment = lax.all_gather(latitude_modes, 'lat', axis=1, tiled=True)]
    all_to_all x1, starting transfers between devices: 9.8 us -> 5.58 us  [per_device(): lax.all_to_all(gridded, 'wave', split_axis=0, concat_axis=2, tiled=True)]
where the time goes in v1:
time: 339 us; the launch traced here: 337 us
  blocking collectives  129 us (38%)
  waiting for transfers between devices  113 us (33%)
  starting transfers between devices  51.6 us (15%)
  local copies, waits for them, and re-layouts  20.4 us (6%)
  other arithmetic  16.1 us (5%)
  matrix products  6.98 us (2%)
    all_to_all x1, blocking collectives, sum_at_owner(): lax.all_to_all(cut_along(array, dim, length), axis, 0, 0, tiled=True)  129 us
    all_to_all x1, waiting for transfers between devices, per_device(): lax.all_to_all(jnp.stack([latitude_modes] * lax.axis_size('lat')), 'lat',...  75.2 us
    ppermute x8, starting transfers between devices, with_halo(): after = lax.ppermute(leading, axis, down)  22.3 us
    all_to_all x1, waiting for transfers between devices, per_device(): lax.all_to_all(gridded, 'wave', split_axis=0, concat_axis=2, tiled=True)  21.3 us
    ppermute x8, waiting for transfers between devices, with_halo(): before = lax.ppermute(last, axis, up)  16.1 us
    ppermute x8, starting transfers between devices, with_halo(): before = lax.ppermute(last, axis, up)  14.2 us
  transfers between devices with their start and end apart: 20, of which 6 were waited for; matrix products, arithmetic and copies ran while one was open for 3% of the time, Pallas kernels for 0%

profile of v1, /device:TPU:64, one launch (start us, length us, event | category | flops | bytes accessed | tf_op | source)
XLA Modules:
  0.0 336.9 jit_solution(12753860186790740476)
XLA Ops:
  0.8 1.4 broadcast_select_fusion
  2.3 4.0 %copy.39 = bf16[40,40,256]{1,0,2:T(8,128)(2,1)} copy(bf16[40,40,256]{2,1,0:T(8,128)(2,1)S(1)} %broadcast_select_fusion) | data formatting | bytes 1638400 | tf_op jit(solution)/shard_map/jit(_where)/select_n | solution.py:106
  6.3 2.7 fusion.7
  9.0 5.8 %copy.41 = bf16[128,2,40,40]{3,2,1,0:T(8,128)(2,1)} copy(bf16[128,2,40,40]{0,2,1,3:T(8,128)(2,1)S(1)} %fusion.7) | data formatting | bytes 1638400 | tf_op jit(solution)/shard_map/convert_element_type | solution.py:110
  14.8 3.2 convolution_convert_fusion
  18.6 128.6 %all_to_all.28 = bf16[16,16,40,256]{3,1,2,0:T(8,128)(2,1)} all-to-all(bf16[16,16,40,256]{3,1,2,0:T(8,128)(2,1)S(1)} %copy.43), channel_id=1, replica_groups=mesh['wave'=16,'lat'=16] {'wave'}, dimensions={0} | all-to-all | bytes 10485760 | tf_op jit(solution)/shard_map/all_to_all | solution.py:19
  147.1 3.3 reduce_sum.12
  150.6 2.9 stack.6
  153.5 4.6 %all-to-all-start.1 = ((bf16[16,16,40,256]{3,2,1,0:T(8,128)(2,1)}), bf16[16,16,40,256]{3,2,1,0:T(8,128)(2,1)}, u32[]{:S(2)}, u32[]{:S(2)}) async-start(bf16[16,16,40,256]{3,2,1,0:T(8,128)(2,1)} %stack.6), calls=%async_computation.1 | async-start | bytes 10485760 | tf_op jit(solution)/shard_map/all_to_all | solution.py:124
  159.1 75.2 %all-to-all-done.1 = bf16[16,16,40,256]{3,2,1,0:T(8,128)(2,1)} async-done(((bf16[16,16,40,256]{3,2,1,0:T(8,128)(2,1)}), bf16[16,16,40,256]{3,2,1,0:T(8,128)(2,1)}, u32[]{:S(2)}, u32[]{:S(2)}) %all-to-all-start.1) | async-done | bytes 5242912 | tf_op jit(solution)/shard_map/all_to_all | solution.py:124
  234.2 3.0 copy.46
  238.3 1.3 copy.47
  239.6 5.6 %all-to-all-start.2 = ((f32[256,80,8]{1,2,0:T(8,128)}), f32[256,80,8]{1,2,0:T(8,128)S(1)}, u32[]{:S(2)}, u32[]{:S(2)}) async-start(f32[256,80,8]{1,2,0:T(8,128)} %copy.47), calls=%async_computation.2 | async-start | bytes 2097152 | tf_op jit(solution)/shard_map/all_to_all | solution.py:130
  246.4 4.9 %collective-permute-start.3 = (f32[1,80,128]{2,1,0:T(8,128)S(1)}, f32[1,80,128]{2,1,0:T(8,128)S(1)}, u32[]{:S(2)}, u32[]{:S(2)}) collective-permute-start(f32[1,80,128]{2,1,0:T(8,128)S(1)} %slice.405), channel_id=1, source_target_pairs={{0,16},{16,32},{32,48},{48,64},{64,80},{80,96},{96,112},{112,128},... | collective-permute-start | bytes 122888 | tf_op jit(solution)/shard_map/ppermute | solution.py:32
  251.3 1.4 convert_multiply_fusion.1
  252.8 21.3 %all-to-all-done.2 = f32[256,80,8]{1,2,0:T(8,128)S(1)} async-done(((f32[256,80,8]{1,2,0:T(8,128)}), f32[256,80,8]{1,2,0:T(8,128)S(1)}, u32[]{:S(2)}, u32[]{:S(2)}) %all-to-all-start.2) | async-done | bytes 655392 | tf_op jit(solution)/shard_map/all_to_all | solution.py:130
  275.2 1.5 copy.52
  277.4 1.9 collective-permute-start.5
  279.3 5.4 %collective-permute-start.4 = (bf16[2,80,128]{2,1,0:T(8,128)(2,1)S(1)}, bf16[2,80,128]{2,1,0:T(8,128)(2,1)S(1)}, u32[]{:S(2)}, u32[]{:S(2)}) collective-permute-start(bf16[2,80,128]{2,1,0:T(8,128)(2,1)S(1)} %get-tuple-element.25), channel_id=1, source_target_pairs={{0,16},{16,32},{32,48},{48,64},{64,80},{80,96},{96,112},{112,128},... | collective-permute-start | bytes 122888 | tf_op jit(solution)/shard_map/ppermute | solution.py:42
  285.6 2.1 collective-permute-done.4
  288.5 2.6 collective-permute-start.7
  291.1 3.6 %collective-permute-start.9 = (bf16[2,80,128]{2,1,0:T(8,128)(2,1)S(1)}, bf16[2,80,128]{2,1,0:T(8,128)(2,1)S(1)}, u32[]{:S(2)}, u32[]{:S(2)}) collective-permute-start(bf16[2,80,128]{2,1,0:T(8,128)(2,1)S(1)} %get-tuple-element.22), channel_id=1, source_target_pairs={{16,0},{32,16},{48,32},{64,48},{80,64},{96,80},{112,96},{128,112},... | collective-permute-start | bytes 122888 | tf_op jit(solution)/shard_map/ppermute | solution.py:43
  294.7 3.8 %collective-permute-start.8 = (bf16[2,80,128]{2,1,0:T(8,128)(2,1)S(1)}, bf16[2,80,128]{2,1,0:T(8,128)(2,1)S(1)}, u32[]{:S(2)}, u32[]{:S(2)}) collective-permute-start(bf16[2,80,128]{2,1,0:T(8,128)(2,1)S(1)} %get-tuple-element.21), channel_id=1, source_target_pairs={{0,16},{16,32},{32,48},{48,64},{64,80},{80,96},{96,112},{112,128},... | collective-permute-start | bytes 122888 | tf_op jit(solution)/shard_map/ppermute | solution.py:42
  299.3 3.7 %collective-permute-done.8 = bf16[2,80,128]{2,1,0:T(8,128)(2,1)S(1)} collective-permute-done((bf16[2,80,128]{2,1,0:T(8,128)(2,1)S(1)}, bf16[2,80,128]{2,1,0:T(8,128)(2,1)S(1)}, u32[]{:S(2)}, u32[]{:S(2)}) %collective-permute-start.8) | collective-permute-done | bytes 40992 | tf_op jit(solution)/shard_map/ppermute | solution.py:42
  303.7 1.9 collective-permute-start.11
  305.6 5.6 %collective-permute-start.13 = (bf16[2,80,128]{2,1,0:T(8,128)(2,1)S(1)}, bf16[2,80,128]{2,1,0:T(8,128)(2,1)S(1)}, u32[]{:S(2)}, u32[]{:S(2)}) collective-permute-start(bf16[2,80,128]{2,1,0:T(8,128)(2,1)S(1)} %get-tuple-element.18), channel_id=1, source_target_pairs={{16,0},{32,16},{48,32},{64,48},{80,64},{96,80},{112,96},{128,112},... | collective-permute-start | bytes 122888 | tf_op jit(solution)/shard_map/ppermute | solution.py:43
  311.3 1.9 collective-permute-start.12
  314.1 5.5 %collective-permute-done.12 = bf16[2,80,128]{2,1,0:T(8,128)(2,1)S(1)} collective-permute-done((bf16[2,80,128]{2,1,0:T(8,128)(2,1)S(1)}, bf16[2,80,128]{2,1,0:T(8,128)(2,1)S(1)}, u32[]{:S(2)}, u32[]{:S(2)}) %collective-permute-start.12) | collective-permute-done | bytes 40992 | tf_op jit(solution)/shard_map/ppermute | solution.py:42
  320.3 1.9 collective-permute-start.15
  322.2 4.8 %collective-permute-start.17 = (bf16[2,80,128]{2,1,0:T(8,128)(2,1)S(1)}, bf16[2,80,128]{2,1,0:T(8,128)(2,1)S(1)}, u32[]{:S(2)}, u32[]{:S(2)}) collective-permute-start(bf16[2,80,128]{2,1,0:T(8,128)(2,1)S(1)} %get-tuple-element.14), channel_id=1, source_target_pairs={{16,0},{32,16},{48,32},{64,48},{80,64},{96,80},{112,96},{128,112},... | collective-permute-start | bytes 122888 | tf_op jit(solution)/shard_map/ppermute | solution.py:43
  327.0 2.6 collective-permute-start.16
  330.5 4.8 %collective-permute-done.16 = bf16[2,80,128]{2,1,0:T(8,128)(2,1)S(1)} collective-permute-done((bf16[2,80,128]{2,1,0:T(8,128)(2,1)S(1)}, bf16[2,80,128]{2,1,0:T(8,128)(2,1)S(1)}, u32[]{:S(2)}, u32[]{:S(2)}) %collective-permute-start.16) | collective-permute-done | bytes 40992 | tf_op jit(solution)/shard_map/ppermute | solution.py:42
  (85 shorter events, 13.6 us)
Async XLA Ops:
  0.0 6.3 %copy-start = (bf16[40,128,128]{2,1,0:T(8,128)(2,1)S(1)}, bf16[40,128,128]{2,1,0:T(8,128)(2,1)}, u32[]{:S(2)}) copy-start(bf16[40,128,128]{2,1,0:T(8,128)(2,1)} %param.9) | copy-start | bytes 3932164
  9.0 5.8 %copy-start.2 = (bf16[40,40,256]{2,1,0:T(8,128)(2,1)S(1)}, bf16[40,40,256]{2,1,0:T(8,128)(2,1)}, u32[]{:S(2)}) copy-start(bf16[40,40,256]{2,1,0:T(8,128)(2,1)} %param.10) | copy-start | bytes 2457604
  153.5 80.7 %all-to-all-start.1 = ((bf16[16,16,40,256]{3,2,1,0:T(8,128)(2,1)}), bf16[16,16,40,256]{3,2,1,0:T(8,128)(2,1)}, u32[]{:S(2)}, u32[]{:S(2)}) async-start(bf16[16,16,40,256]{3,2,1,0:T(8,128)(2,1)} %stack.6), calls=%async_computation.1 | async-start | bytes 10485760 | tf_op jit(solution)/shard_map/all_to_all | solution.py:124
  238.3 6.9 %copy-start.3 = (f32[16,80,128]{2,1,0:T(8,128)S(1)}, f32[16,80,128]{2,1,0:T(8,128)}, u32[]{:S(2)}) copy-start(f32[16,80,128]{2,1,0:T(8,128)} %param.13) | copy-start | bytes 1966084
  239.6 34.5 %all-to-all-start.2 = ((f32[256,80,8]{1,2,0:T(8,128)}), f32[256,80,8]{1,2,0:T(8,128)S(1)}, u32[]{:S(2)}, u32[]{:S(2)}) async-start(f32[256,80,8]{1,2,0:T(8,128)} %copy.47), calls=%async_computation.2 | async-start | bytes 2097152 | tf_op jit(solution)/shard_map/all_to_all | solution.py:130
  246.4 41.6 %collective-permute-start.3 = (f32[1,80,128]{2,1,0:T(8,128)S(1)}, f32[1,80,128]{2,1,0:T(8,128)S(1)}, u32[]{:S(2)}, u32[]{:S(2)}) collective-permute-start(f32[1,80,128]{2,1,0:T(8,128)S(1)} %slice.405), channel_id=1, source_target_pairs={{0,16},{16,32},{32,48},{48,64},{64,80},{80,96},{96,112},{112,128},... | collective-permute-start | bytes 122888 | tf_op jit(solution)/shard_map/ppermute | solution.py:32
  252.7 32.5 %collective-permute-start = (f32[16,1,128]{2,0,1:T(8,128)S(1)}, f32[16,1,128]{2,0,1:T(8,128)S(1)}, u32[]{:S(2)}, u32[]{:S(2)}) collective-permute-start(f32[16,1,128]{2,0,1:T(8,128)S(1)} %bitcast.44), channel_id=1, source_target_pairs={{0,1},{1,2},{2,3},{3,4},{4,5},{5,6},{6,7},{7,8},{8,9},{9,10},{10,1... | collective-permute-start | bytes 24584 | tf_op jit(solution)/shard_map/ppermute | solution.py:26
  276.8 2.5 collective-permute-start.2
  276.9 7.9 %collective-permute-start.1 = (bf16[16,2,128]{2,1,0:T(2,128)(2,1)S(1)}, bf16[16,2,128]{2,1,0:T(2,128)(2,1)S(1)}, u32[]{:S(2)}, u32[]{:S(2)}) collective-permute-start(bf16[16,2,128]{2,1,0:T(2,128)(2,1)S(1)} %get-tuple-element.23), channel_id=1, source_target_pairs={{0,1},{1,2},{2,3},{3,4},{4,5},{5,6},{6,7},{7,8},{8,9},{9,10},{10,1... | collective-permute-start | bytes 24584 | tf_op jit(solution)/shard_map/ppermute | solution.py:42
  277.4 8.2 %collective-permute-start.5 = (bf16[2,80,128]{2,1,0:T(8,128)(2,1)S(1)}, bf16[2,80,128]{2,1,0:T(8,128)(2,1)S(1)}, u32[]{:S(2)}, u32[]{:S(2)}) collective-permute-start(bf16[2,80,128]{2,1,0:T(8,128)(2,1)S(1)} %get-tuple-element.26), channel_id=1, source_target_pairs={{16,0},{32,16},{48,32},{64,48},{80,64},{96,80},{112,96},{128,112},... | collective-permute-start | bytes 122888 | tf_op jit(solution)/shard_map/ppermute | solution.py:43
  279.3 8.4 %collective-permute-start.4 = (bf16[2,80,128]{2,1,0:T(8,128)(2,1)S(1)}, bf16[2,80,128]{2,1,0:T(8,128)(2,1)S(1)}, u32[]{:S(2)}, u32[]{:S(2)}) collective-permute-start(bf16[2,80,128]{2,1,0:T(8,128)(2,1)S(1)} %get-tuple-element.25), channel_id=1, source_target_pairs={{0,16},{16,32},{32,48},{48,64},{64,80},{80,96},{96,112},{112,128},... | collective-permute-start | bytes 122888 | tf_op jit(solution)/shard_map/ppermute | solution.py:42
  288.5 9.9 %collective-permute-start.7 = (bf16[16,2,128]{2,1,0:T(2,128)(2,1)S(1)}, bf16[16,2,128]{2,1,0:T(2,128)(2,1)S(1)}, u32[]{:S(2)}, u32[]{:S(2)}) collective-permute-start(bf16[16,2,128]{2,1,0:T(2,128)(2,1)S(1)} %get-tuple-element.20), channel_id=1, source_target_pairs={{1,0},{2,1},{3,2},{4,3},{5,4},{6,5},{7,6},{8,7},{9,8},{10,9},{11,1... | collective-permute-start | bytes 24584 | tf_op jit(solution)/shard_map/ppermute | solution.py:43
  291.1 7.4 %collective-permute-start.6 = (bf16[16,2,128]{2,1,0:T(2,128)(2,1)S(1)}, bf16[16,2,128]{2,1,0:T(2,128)(2,1)S(1)}, u32[]{:S(2)}, u32[]{:S(2)}) collective-permute-start(bf16[16,2,128]{2,1,0:T(2,128)(2,1)S(1)} %get-tuple-element.19), channel_id=1, source_target_pairs={{0,1},{1,2},{2,3},{3,4},{4,5},{5,6},{6,7},{7,8},{8,9},{9,10},{10,1... | collective-permute-start | bytes 24584 | tf_op jit(solution)/shard_map/ppermute | solution.py:42
  291.1 8.2 %collective-permute-start.9 = (bf16[2,80,128]{2,1,0:T(8,128)(2,1)S(1)}, bf16[2,80,128]{2,1,0:T(8,128)(2,1)S(1)}, u32[]{:S(2)}, u32[]{:S(2)}) collective-permute-start(bf16[2,80,128]{2,1,0:T(8,128)(2,1)S(1)} %get-tuple-element.22), channel_id=1, source_target_pairs={{16,0},{32,16},{48,32},{64,48},{80,64},{96,80},{112,96},{128,112},... | collective-permute-start | bytes 122888 | tf_op jit(solution)/shard_map/ppermute | solution.py:43
  294.7 8.3 %collective-permute-start.8 = (bf16[2,80,128]{2,1,0:T(8,128)(2,1)S(1)}, bf16[2,80,128]{2,1,0:T(8,128)(2,1)S(1)}, u32[]{:S(2)}, u32[]{:S(2)}) collective-permute-start(bf16[2,80,128]{2,1,0:T(8,128)(2,1)S(1)} %get-tuple-element.21), channel_id=1, source_target_pairs={{0,16},{16,32},{32,48},{48,64},{64,80},{80,96},{96,112},{112,128},... | collective-permute-start | bytes 122888 | tf_op jit(solution)/shard_map/ppermute | solution.py:42
  303.7 9.5 %collective-permute-start.11 = (bf16[16,2,128]{2,1,0:T(2,128)(2,1)S(1)}, bf16[16,2,128]{2,1,0:T(2,128)(2,1)S(1)}, u32[]{:S(2)}, u32[]{:S(2)}) collective-permute-start(bf16[16,2,128]{2,1,0:T(2,128)(2,1)S(1)} %get-tuple-element.16), channel_id=1, source_target_pairs={{1,0},{2,1},{3,2},{4,3},{5,4},{6,5},{7,6},{8,7},{9,8},{10,9},{11,1... | collective-permute-start | bytes 24584 | tf_op jit(solution)/shard_map/ppermute | solution.py:43
  305.6 7.6 %collective-permute-start.10 = (bf16[16,2,128]{2,1,0:T(2,128)(2,1)S(1)}, bf16[16,2,128]{2,1,0:T(2,128)(2,1)S(1)}, u32[]{:S(2)}, u32[]{:S(2)}) collective-permute-start(bf16[16,2,128]{2,1,0:T(2,128)(2,1)S(1)} %get-tuple-element.15), channel_id=1, source_target_pairs={{0,1},{1,2},{2,3},{3,4},{4,5},{5,6},{6,7},{7,8},{8,9},{9,10},{10,1... | collective-permute-start | bytes 24584 | tf_op jit(solution)/shard_map/ppermute | solution.py:42
  305.6 8.4 %collective-permute-start.13 = (bf16[2,80,128]{2,1,0:T(8,128)(2,1)S(1)}, bf16[2,80,128]{2,1,0:T(8,128)(2,1)S(1)}, u32[]{:S(2)}, u32[]{:S(2)}) collective-permute-start(bf16[2,80,128]{2,1,0:T(8,128)(2,1)S(1)} %get-tuple-element.18), channel_id=1, source_target_pairs={{16,0},{32,16},{48,32},{64,48},{80,64},{96,80},{112,96},{128,112},... | collective-permute-start | bytes 122888 | tf_op jit(solution)/shard_map/ppermute | solution.py:43
  311.3 8.3 %collective-permute-start.12 = (bf16[2,80,128]{2,1,0:T(8,128)(2,1)S(1)}, bf16[2,80,128]{2,1,0:T(8,128)(2,1)S(1)}, u32[]{:S(2)}, u32[]{:S(2)}) collective-permute-start(bf16[2,80,128]{2,1,0:T(8,128)(2,1)S(1)} %get-tuple-element.17), channel_id=1, source_target_pairs={{0,16},{16,32},{32,48},{48,64},{64,80},{80,96},{96,112},{112,128},... | collective-permute-start | bytes 122888 | tf_op jit(solution)/shard_map/ppermute | solution.py:42
  320.3 9.3 %collective-permute-start.15 = (bf16[16,2,128]{2,1,0:T(2,128)(2,1)S(1)}, bf16[16,2,128]{2,1,0:T(2,128)(2,1)S(1)}, u32[]{:S(2)}, u32[]{:S(2)}) collective-permute-start(bf16[16,2,128]{2,1,0:T(2,128)(2,1)S(1)} %get-tuple-element.12), channel_id=1, source_target_pairs={{1,0},{2,1},{3,2},{4,3},{5,4},{6,5},{7,6},{8,7},{9,8},{10,9},{11,1... | collective-permute-start | bytes 24584 | tf_op jit(solution)/shard_map/ppermute | solution.py:43
  322.2 7.4 %collective-permute-start.14 = (bf16[16,2,128]{2,1,0:T(2,128)(2,1)S(1)}, bf16[16,2,128]{2,1,0:T(2,128)(2,1)S(1)}, u32[]{:S(2)}, u32[]{:S(2)}) collective-permute-start(bf16[16,2,128]{2,1,0:T(2,128)(2,1)S(1)} %get-tuple-element.11), channel_id=1, source_target_pairs={{0,1},{1,2},{2,3},{3,4},{4,5},{5,6},{6,7},{7,8},{8,9},{9,10},{10,1... | collective-permute-start | bytes 24584 | tf_op jit(solution)/shard_map/ppermute | solution.py:42
  322.2 8.2 %collective-permute-start.17 = (bf16[2,80,128]{2,1,0:T(8,128)(2,1)S(1)}, bf16[2,80,128]{2,1,0:T(8,128)(2,1)S(1)}, u32[]{:S(2)}, u32[]{:S(2)}) collective-permute-start(bf16[2,80,128]{2,1,0:T(8,128)(2,1)S(1)} %get-tuple-element.14), channel_id=1, source_target_pairs={{16,0},{32,16},{48,32},{64,48},{80,64},{96,80},{112,96},{128,112},... | collective-permute-start | bytes 122888 | tf_op jit(solution)/shard_map/ppermute | solution.py:43
  327.0 8.3 %collective-permute-start.16 = (bf16[2,80,128]{2,1,0:T(8,128)(2,1)S(1)}, bf16[2,80,128]{2,1,0:T(8,128)(2,1)S(1)}, u32[]{:S(2)}, u32[]{:S(2)}) collective-permute-start(bf16[2,80,128]{2,1,0:T(8,128)(2,1)S(1)} %get-tuple-element.13), channel_id=1, source_target_pairs={{0,16},{16,32},{32,48},{48,64},{64,80},{80,96},{96,112},{112,128},... | collective-permute-start | bytes 122888 | tf_op jit(solution)/shard_map/ppermute | solution.py:42
  335.6 1.3 copy-start.1
